TPU v7x, 32 devices: a whole 2x2x4 slice. The times are simulated.
32 devices in a mesh: seq: 4 (over x, core), fsdp: 8 (over z, y).
Axes of the slice: x: 2, y: 2, z: 4, core: 2. Of those that a mesh axis runs over, the one named last changes fastest.
Arguments:
- tokens: bfloat16 [8, 1024, 2048], P('fsdp', 'seq'), may hold values from -6 to 6
- targets: bfloat16 [8, 1024, 2048], P('fsdp', 'seq'), may hold values from -6 to 6
- lengths: int32 [8], replicated, may hold values from 1 to 1024, 6144 in all
- w_qkv: float32 [2048, 3, 2048], P('fsdp', None, 'seq'), may hold values from -0.125 to 0.125
- w_out: float32 [2048, 2048], P('seq', 'fsdp'), may hold values from -1 to 1
- w_gateup: float32 [2048, 2, 8192], P('fsdp', None, 'seq'), may hold values from -0.125 to 0.125
- w_down: float32 [8192, 2048], P('seq', 'fsdp'), may hold values from -0.0625 to 0.0625
- mom_qkv: float32 [2048, 3, 2048], P('fsdp', None, 'seq'), may hold values from -0.0390625 to 0.0390625
- mom_out: float32 [2048, 2048], P('seq', 'fsdp'), may hold values from -0.0234375 to 0.0234375
- mom_gateup: float32 [2048, 2, 8192], P('fsdp', None, 'seq'), may hold values from -0.0390625 to 0.0390625
- mom_down: float32 [8192, 2048], P('seq', 'fsdp'), may hold values from -0.078125 to 0.078125
- avg_qkv: float32 [2048, 3, 2048], P('fsdp', None, 'seq'), may hold values from -0.125 to 0.125
- avg_out: float32 [2048, 2048], P('seq', 'fsdp'), may hold values from -1 to 1
- avg_gateup: float32 [2048, 2, 8192], P('fsdp', None, 'seq'), may hold values from -0.125 to 0.125
- avg_down: float32 [8192, 2048], P('seq', 'fsdp'), may hold values from -0.0625 to 0.0625
Outputs:
- output: bfloat16 [8, 1024, 2048], P('fsdp', 'seq')
- input_grad: bfloat16 [8, 1024, 2048], P('fsdp', 'seq')
- loss: float32 [], replicated
- new_qkv: float32 [2048, 3, 2048], P('fsdp', None, 'seq')
- new_out: float32 [2048, 2048], P('seq', 'fsdp')
- new_gateup: float32 [2048, 2, 8192], P('fsdp', None, 'seq')
- new_down: float32 [8192, 2048], P('seq', 'fsdp')
- newmom_qkv: float32 [2048, 3, 2048], P('fsdp', None, 'seq')
- newmom_out: float32 [2048, 2048], P('seq', 'fsdp')
- newmom_gateup: float32 [2048, 2, 8192], P('fsdp', None, 'seq')
- newmom_down: float32 [8192, 2048], P('seq', 'fsdp')
- newavg_qkv: float32 [2048, 3, 2048], P('fsdp', None, 'seq')
- newavg_out: float32 [2048, 2048], P('seq', 'fsdp')
- newavg_gateup: float32 [2048, 2, 8192], P('fsdp', None, 'seq')
- newavg_down: float32 [8192, 2048], P('seq', 'fsdp')
Inputs may be any that keep to these rules, and one draw needn't show every extreme that they name: lengths[s] valid tokens stand first in sequence s's 1024 slots, padding after; they sum to 6144 and one equals 1024.
All inputs are finite; a program needn't handle non-finite values.
Results may differ from a plain program's by a relative error of at most 0.015.
Values may be sent and summed in bfloat16 or wider, within the bound.
A program may use at most 256 MiB of HBM per device.

v0:
```python
import jax
import jax.numpy as jnp
from jax import lax
from jax.sharding import PartitionSpec as P

HD = 128
EPS = 1e-05
ROPE_BASE = 10000.0
MOMENT = 0.9
KEEP = 0.95
NEG = -1e30


def layer_norm(values):
    centred = values - jnp.mean(values, axis=-1, keepdims=True)
    factor = lax.rsqrt(jnp.mean(centred * centred, axis=-1, keepdims=True) + EPS)
    return (centred * factor, factor)


def norm_back(grad, normed, factor):
    inner = jnp.mean(grad * normed, axis=-1, keepdims=True)
    return factor * (grad - jnp.mean(grad, axis=-1, keepdims=True) - normed * inner)


def rotary(span, width):
    half = width // 2
    freq = ROPE_BASE ** (-2.0 * jnp.arange(half, dtype=jnp.float32) / width)
    angle = jnp.arange(span, dtype=jnp.float32)[:, None] * freq[None, :]
    cosine = jnp.concatenate([jnp.cos(angle), jnp.cos(angle)], axis=-1)[:, None, :]
    sine = jnp.concatenate([jnp.sin(angle), jnp.sin(angle)], axis=-1)[:, None, :]
    return (cosine, sine)


def rotate(values):
    half = values.shape[-1] // 2
    return jnp.concatenate([-values[..., half:], values[..., :half]], axis=-1)


def unrotate(values):
    half = values.shape[-1] // 2
    return jnp.concatenate([values[..., half:], -values[..., :half]], axis=-1)


def allowed_mask(first_row, block_rows, span, length):
    positions = jnp.arange(span, dtype=jnp.int32)
    query_pos = first_row + jnp.arange(block_rows, dtype=jnp.int32)
    return (positions[None, :] <= query_pos[:, None]) & (positions[None, :] < length)


def attend_forward(queries, keys_rot, values_v, length):
    span = queries.shape[0]
    block_rows = min(512, span)
    scale = queries.shape[2] ** (-0.5)

    def one_block(first_row):
        rows_q = lax.dynamic_slice_in_dim(queries, first_row, block_rows, 0)
        scores = (
            jnp.einsum("qhd,khd->hqk", rows_q, keys_rot, preferred_element_type=jnp.float32) * scale
        )
        scores = jnp.where(allowed_mask(first_row, block_rows, span, length)[None], scores, NEG)
        highest = jnp.max(scores, axis=-1, keepdims=True)
        expvals = jnp.exp(scores - highest)
        totals = jnp.sum(expvals, axis=-1, keepdims=True)
        attn_probs = (expvals / totals).astype(jnp.bfloat16)
        outs = jnp.einsum("hqk,khd->qhd", attn_probs, values_v, preferred_element_type=jnp.float32)
        return (outs, highest[..., 0] + jnp.log(totals[..., 0]))

    starts = jnp.arange(span // block_rows) * block_rows
    outs, log_totals = lax.map(one_block, starts)
    return (outs.reshape(span, queries.shape[1], queries.shape[2]), log_totals)


def attend_back(queries, keys_rot, values_v, grad_out, log_totals, length):
    span = queries.shape[0]
    block_rows = min(512, span)
    scale = queries.shape[2] ** (-0.5)
    starts = jnp.arange(span // block_rows) * block_rows

    def one_block(carry, item):
        first_row, lse_block = item
        rows_q = lax.dynamic_slice_in_dim(queries, first_row, block_rows, 0)
        rows_g = lax.dynamic_slice_in_dim(grad_out, first_row, block_rows, 0)
        scores = (
            jnp.einsum("qhd,khd->hqk", rows_q, keys_rot, preferred_element_type=jnp.float32) * scale
        )
        allowed = allowed_mask(first_row, block_rows, span, length)[None]
        attn_probs = jnp.where(allowed, jnp.exp(scores - lse_block[..., None]), 0.0)
        probs_low = attn_probs.astype(jnp.bfloat16)
        grad_values = carry[1] + jnp.einsum(
            "hqk,qhd->khd", probs_low, rows_g, preferred_element_type=jnp.float32
        )
        grad_probs = jnp.einsum(
            "qhd,khd->hqk", rows_g, values_v, preferred_element_type=jnp.float32
        )
        inner = jnp.sum(attn_probs * grad_probs, axis=-1, keepdims=True)
        grad_scores = (attn_probs * (grad_probs - inner)).astype(jnp.bfloat16)
        grad_rows = (
            jnp.einsum("hqk,khd->qhd", grad_scores, keys_rot, preferred_element_type=jnp.float32)
            * scale
        )
        grad_keys = (
            carry[0]
            + jnp.einsum("hqk,qhd->khd", grad_scores, rows_q, preferred_element_type=jnp.float32)
            * scale
        )
        return ((grad_keys, grad_values), grad_rows)

    zeros_kv = jnp.zeros(keys_rot.shape, jnp.float32)
    (grad_keys, grad_values), grad_rows = lax.scan(
        one_block, (zeros_kv, zeros_kv), (starts, log_totals)
    )
    return (grad_rows.reshape(queries.shape), grad_keys, grad_values)


def advance(weight, moment, average, grad, rate):
    moment_new = MOMENT * moment + grad
    weight_new = weight - rate * (grad + MOMENT * moment_new)
    average_new = KEEP * average + (1.0 - KEEP) * weight_new
    return (weight_new, moment_new, average_new)


def on_device(
    tokens,
    targets,
    lengths,
    w_qkv,
    w_out,
    w_gateup,
    w_down,
    mom_qkv,
    mom_out,
    mom_gateup,
    mom_down,
    avg_qkv,
    avg_out,
    avg_gateup,
    avg_down,
):
    n_shards = lax.axis_size("seq")
    shard_index = lax.axis_index("seq")
    member = lax.axis_index("fsdp")
    own_rows = tokens.shape[1]
    span = own_rows * n_shards
    head_size = HD
    heads_here = w_qkv.shape[2] // head_size
    inputs = tokens[0].astype(jnp.float32)
    target = targets[0].astype(jnp.float32)
    own_length = lax.dynamic_index_in_dim(lengths, member, 0, keepdims=False)
    count = jnp.sum(lengths).astype(jnp.float32)
    own_pos = shard_index * own_rows + jnp.arange(own_rows, dtype=jnp.int32)
    valid = (own_pos < own_length).astype(jnp.float32)[:, None]
    low_weights = (
        w_qkv.astype(jnp.bfloat16),
        w_out.astype(jnp.bfloat16),
        w_gateup.astype(jnp.bfloat16),
        w_down.astype(jnp.bfloat16),
    )
    full_qkv, full_out, full_gateup, full_down = (
        lax.all_gather(low_weights[0], "fsdp", axis=0, tiled=True),
        lax.all_gather(low_weights[1], "fsdp", axis=1, tiled=True),
        lax.all_gather(low_weights[2], "fsdp", axis=0, tiled=True),
        lax.all_gather(low_weights[3], "fsdp", axis=1, tiled=True),
    )
    normed_one, factor_one = layer_norm(inputs)
    group_one = lax.all_gather(normed_one.astype(jnp.bfloat16), "seq", axis=0, tiled=True)
    qkv_all = jnp.einsum("td,djc->tjc", group_one, full_qkv, preferred_element_type=jnp.float32)
    cosine, sine = rotary(span, head_size)
    queries = qkv_all[:, 0].reshape(span, heads_here, head_size)
    keys_pre = qkv_all[:, 1].reshape(span, heads_here, head_size)
    queries = (queries * cosine + rotate(queries) * sine).astype(jnp.bfloat16)
    keys_rot = (keys_pre * cosine + rotate(keys_pre) * sine).astype(jnp.bfloat16)
    values_v = qkv_all[:, 2].reshape(span, heads_here, head_size).astype(jnp.bfloat16)
    attended, log_totals = attend_forward(queries, keys_rot, values_v, own_length)
    attended = attended.reshape(span, heads_here * head_size).astype(jnp.bfloat16)
    attn_term = jnp.dot(attended, full_out, preferred_element_type=jnp.float32)
    middle = inputs + lax.psum_scatter(
        attn_term.astype(jnp.bfloat16), "seq", scatter_dimension=0, tiled=True
    ).astype(jnp.float32)
    normed_two, factor_two = layer_norm(middle)
    group_two = lax.all_gather(normed_two.astype(jnp.bfloat16), "seq", axis=0, tiled=True)
    gate_up = jnp.einsum("td,djf->tjf", group_two, full_gateup, preferred_element_type=jnp.float32)
    gate = gate_up[:, 0]
    up_part = gate_up[:, 1]
    hidden = (jax.nn.silu(gate) * up_part).astype(jnp.bfloat16)
    ffn_term = jnp.dot(hidden, full_down, preferred_element_type=jnp.float32)
    result = middle + lax.psum_scatter(
        ffn_term.astype(jnp.bfloat16), "seq", scatter_dimension=0, tiled=True
    ).astype(jnp.float32)
    diff = (result - target) * valid
    loss = lax.psum(jnp.sum(diff * diff), ("seq", "fsdp")) / (2.0 * count)
    grad_result = diff / count
    full_qkv, full_out, full_gateup, full_down = (
        lax.all_gather(low_weights[0], "fsdp", axis=0, tiled=True),
        lax.all_gather(low_weights[1], "fsdp", axis=1, tiled=True),
        lax.all_gather(low_weights[2], "fsdp", axis=0, tiled=True),
        lax.all_gather(low_weights[3], "fsdp", axis=1, tiled=True),
    )
    contract_rows = (((0,), (0,)), ((), ()))
    contract_cols = (((1,), (1,)), ((), ()))
    group_dy = lax.all_gather(grad_result.astype(jnp.bfloat16), "seq", axis=0, tiled=True)
    grad_hidden = lax.dot_general(
        group_dy, full_down, contract_cols, preferred_element_type=jnp.float32
    )
    grad_down = lax.dot_general(hidden, group_dy, contract_rows, preferred_element_type=jnp.float32)
    sigma = jax.nn.sigmoid(gate)
    grad_gate = grad_hidden * up_part * sigma * (1.0 + gate * (1.0 - sigma))
    grad_up = grad_hidden * gate * sigma
    grad_gu = jnp.stack([grad_gate, grad_up], axis=1).astype(jnp.bfloat16)
    normed_grad_two = jnp.einsum(
        "tjf,djf->td", grad_gu, full_gateup, preferred_element_type=jnp.float32
    )
    grad_gateup = jnp.einsum("td,tjf->djf", group_two, grad_gu, preferred_element_type=jnp.float32)
    own_grad_two = lax.psum_scatter(
        normed_grad_two.astype(jnp.bfloat16), "seq", scatter_dimension=0, tiled=True
    ).astype(jnp.float32)
    grad_middle = grad_result + norm_back(own_grad_two, normed_two, factor_two)
    group_da = lax.all_gather(grad_middle.astype(jnp.bfloat16), "seq", axis=0, tiled=True)
    grad_att = lax.dot_general(
        group_da, full_out, contract_cols, preferred_element_type=jnp.float32
    )
    grad_att = grad_att.astype(jnp.bfloat16).reshape(span, heads_here, head_size)
    grad_out = lax.dot_general(
        attended, group_da, contract_rows, preferred_element_type=jnp.float32
    )
    grad_rows, grad_keys, grad_values = attend_back(
        queries, keys_rot, values_v, grad_att, log_totals, own_length
    )
    grad_rows = grad_rows * cosine + unrotate(grad_rows * sine)
    grad_keys = grad_keys * cosine + unrotate(grad_keys * sine)
    grad_qkv_all = jnp.stack(
        [grad_rows.reshape(span, -1), grad_keys.reshape(span, -1), grad_values.reshape(span, -1)],
        axis=1,
    ).astype(jnp.bfloat16)
    normed_grad_one = jnp.einsum(
        "tjc,djc->td", grad_qkv_all, full_qkv, preferred_element_type=jnp.float32
    )
    grad_qkv = jnp.einsum(
        "td,tjc->djc", group_one, grad_qkv_all, preferred_element_type=jnp.float32
    )
    own_grad_one = lax.psum_scatter(
        normed_grad_one.astype(jnp.bfloat16), "seq", scatter_dimension=0, tiled=True
    ).astype(jnp.float32)
    grad_inputs = grad_middle + norm_back(own_grad_one, normed_one, factor_one)
    summed_qkv, summed_out, summed_gateup, summed_down = (
        lax.psum_scatter(
            grad_qkv.astype(jnp.bfloat16), "fsdp", scatter_dimension=0, tiled=True
        ).astype(jnp.float32),
        lax.psum_scatter(
            grad_out.astype(jnp.bfloat16), "fsdp", scatter_dimension=1, tiled=True
        ).astype(jnp.float32),
        lax.psum_scatter(
            grad_gateup.astype(jnp.bfloat16), "fsdp", scatter_dimension=0, tiled=True
        ).astype(jnp.float32),
        lax.psum_scatter(
            grad_down.astype(jnp.bfloat16), "fsdp", scatter_dimension=1, tiled=True
        ).astype(jnp.float32),
    )
    new_qkv, newmom_qkv, newavg_qkv = advance(w_qkv, mom_qkv, avg_qkv, summed_qkv, 2.0)
    new_out, newmom_out, newavg_out = advance(w_out, mom_out, avg_out, summed_out, 20.0)
    new_gateup, newmom_gateup, newavg_gateup = advance(
        w_gateup, mom_gateup, avg_gateup, summed_gateup, 2.0
    )
    new_down, newmom_down, newavg_down = advance(w_down, mom_down, avg_down, summed_down, 1.0)
    return (
        result.astype(jnp.bfloat16)[None],
        grad_inputs.astype(jnp.bfloat16)[None],
        loss,
        new_qkv,
        new_out,
        new_gateup,
        new_down,
        newmom_qkv,
        newmom_out,
        newmom_gateup,
        newmom_down,
        newavg_qkv,
        newavg_out,
        newavg_gateup,
        newavg_down,
    )


def solution(mesh):
    placed = (
        P("fsdp", "seq", None),
        P("fsdp", "seq", None),
        P(),
        P("fsdp", None, "seq"),
        P("seq", "fsdp"),
        P("fsdp", None, "seq"),
        P("seq", "fsdp"),
        P("fsdp", None, "seq"),
        P("seq", "fsdp"),
        P("fsdp", None, "seq"),
        P("seq", "fsdp"),
        P("fsdp", None, "seq"),
        P("seq", "fsdp"),
        P("fsdp", None, "seq"),
        P("seq", "fsdp"),
    )
    return jax.shard_map(
        on_device,
        mesh=mesh,
        in_specs=placed,
        out_specs=(
            P("fsdp", "seq", None),
            P("fsdp", "seq", None),
            P(),
            P("fsdp", None, "seq"),
            P("seq", "fsdp"),
            P("fsdp", None, "seq"),
            P("seq", "fsdp"),
            P("fsdp", None, "seq"),
            P("seq", "fsdp"),
            P("fsdp", None, "seq"),
            P("seq", "fsdp"),
            P("fsdp", None, "seq"),
            P("seq", "fsdp"),
            P("fsdp", None, "seq"),
            P("seq", "fsdp"),
        ),
        check_vma=False,
    )
```

profile of v0, /device:TPU:0, one launch (start us, length us, event | category | flops | bytes accessed | tf_op | source)
XLA Modules:
  0.0 1588.2 jit_solution(3938071013215438621)
XLA Ops:
  19.5 30.2 %all-gather.9.cloned.1.call-done = bf16[1024,2048]{1,0:T(8,128)(2,1)} async-done(((bf16[256,2048]{1,0:T(8,128)(2,1)}), bf16[1024,2048]{1,0:T(8,128)(2,1)}) %all-gather.9.cloned.1.call-update) | async-done | bytes 4194320 | tf_op jit(solution)/shard_map/all_gather | solution.py:165
  49.7 102.1 %all-gather.11.cloned.1.call-done = bf16[2048,3,512]{0,2,1:T(8,128)(2,1)} async-done(((bf16[256,3,512]{0,2,1:T(8,128)(2,1)}), bf16[2048,3,512]{0,2,1:T(8,128)(2,1)}) %all-gather.11.cloned.1.call-update) | async-done | bytes 6291472 | tf_op jit(solution)/shard_map/all_gather | solution.py:159
  180.4 24.5 %while.29 = (s32[]{:T(128)}, bf16[2,512,4,128]{3,1,2,0:T(8,128)(2,1)}, f32[2,4,512]{2,1,0:T(4,128)S(1)}, s32[2]{0:T(128)S(1)}, s32[]{:T(128)}, /*index=5*/bf16[1...) while((s32[]{:T(128)}, ...), condition=%wide.region_5.6_spmd.clone, body=%wide.region_2.5_spmd.sunk.clone | while | flops 1099955712 | bytes 35199660 | solution.py:69
  215.1 42.9 %reduce-scatter.9.cloned.1.call-done = bf16[256,2048]{1,0:T(8,128)(2,1)} async-done(((bf16[1024,2048]{1,0:T(8,128)(2,1)}), bf16[256,2048]{1,0:T(8,128)(2,1)}) %reduce-scatter.9.cloned.1.call-update) | async-done | bytes 1048592 | tf_op jit(solution)/shard_map/reduce_scatter | solution.py:176
  270.4 25.8 %all-gather.15.cloned.1.call-done = bf16[1024,2048]{1,0:T(8,128)(2,1)} async-done(((bf16[256,2048]{1,0:T(8,128)(2,1)}), bf16[1024,2048]{1,0:T(8,128)(2,1)}) %all-gather.15.cloned.1.call-update) | async-done | bytes 4194320 | tf_op jit(solution)/shard_map/all_gather | solution.py:180
  296.2 229.9 %all-gather.17.cloned.1.call-done = bf16[2048,2,2048]{2,0,1:T(8,128)(2,1)} async-done(((bf16[256,2,2048]{2,0,1:T(8,128)(2,1)}), bf16[2048,2,2048]{2,0,1:T(8,128)(2,1)}) %all-gather.17.cloned.1.call-update) | async-done | bytes 16777232 | tf_op jit(solution)/shard_map/all_gather | solution.py:161
  526.1 21.5 %fusion.39 = f32[1024,2,2048]{2,0,1:T(8,128)S(1)} fusion(bf16[2048,2,2048]{2,0,1:T(8,128)(2,1)} %all-gather.17.cloned.1.call-done, bf16[1024,2048]{1,0:T(8,128)(2,1)} %all-gather.15.cloned.1.call-done), kind=kOutput, calls=%fused_computation.67 | convolution fusion | flops 17179869184 | bytes 37748736 | tf_op jit(solution)/shard_map/td,djf->tjf/dot_general | solution.py:181
  557.2 94.6 %all-gather.19.cloned.1.call-done = bf16[2048,2048]{1,0:T(8,128)(2,1)} async-done(((bf16[2048,256]{1,0:T(8,128)(2,1)}), bf16[2048,2048]{1,0:T(8,128)(2,1)}) %all-gather.19.cloned.1.call-update) | async-done | bytes 8388624 | tf_op jit(solution)/shard_map/all_gather | solution.py:162
  651.9 13.8 convolution_convert_fusion.3
  668.2 40.4 %reduce-scatter.11.cloned.1.call-done = bf16[256,2048]{1,0:T(8,128)(2,1)} async-done(((bf16[1024,2048]{1,0:T(8,128)(2,1)}), bf16[256,2048]{1,0:T(8,128)(2,1)}) %reduce-scatter.11.cloned.1.call-update) | async-done | bytes 1048592 | tf_op jit(solution)/shard_map/reduce_scatter | solution.py:186
  711.7 34.6 %all-gather.21.cloned.1.call-done = bf16[1024,2048]{1,0:T(8,128)(2,1)} async-done(((bf16[256,2048]{1,0:T(8,128)(2,1)}), bf16[1024,2048]{1,0:T(8,128)(2,1)}) %all-gather.21.cloned.1.call-update) | async-done | bytes 4194320 | tf_op jit(solution)/shard_map/all_gather | solution.py:200
  746.2 20.5 %fusion.46 = (bf16[1024,1,2048]{2,0,1:T(8,128)(2,1)}, bf16[1024,1,2048]{2,0,1:T(8,128)(2,1)}) fusion(f32[1024,2,2048]{2,0,1:T(8,128)} %copy-done.16, bf16[1024,2048]{1,0:T(8,128)(2,1)} %all-gather.21.cloned.1.call-done, bf16[2048,2048]{1,0:T(8,128)(2,1)} %all-gather.19.cloned.1.call-done), kind=kOutput, calls=%fused_computation.76 | convolution fusion | flops 8617197568 | bytes 37748736 | tf_op jit(solution)/shard_map/dot_general | solution.py:201
  766.7 23.9 %bitcast_convert_fusion.1 = bf16[1024,2048]{1,0:T(8,128)(2,1)} fusion(bf16[2048,2,2048]{2,0,1:T(8,128)(2,1)} %all-gather.17.cloned.1.call-done, bf16[1024,1,2048]{2,0,1:T(8,128)(2,1)} %get-tuple-element.287, bf16[1024,1,2048]{2,0,1:T(8,128)(2,1)} %get-tuple-element.286), kind=kOutput, calls=%fused_computation.54 | convolution fusion | flops 17186160640 | bytes 29360128 | tf_op jit(solution)/shard_map/tjf,djf->td/dot_general | solution.py:209
  790.7 44.7 %reduce-scatter.13.cloned.1.call-done = bf16[256,2048]{1,0:T(8,128)(2,1)} async-done(((bf16[1024,2048]{1,0:T(8,128)(2,1)}), bf16[256,2048]{1,0:T(8,128)(2,1)}) %reduce-scatter.13.cloned.1.call-update) | async-done | bytes 1048592 | tf_op jit(solution)/shard_map/reduce_scatter | solution.py:213
  842.8 14.5 convolution_convert_fusion.1
  863.2 14.2 all-gather.23.cloned.1.call-done
  889.7 52.0 %while.30 = (s32[]{:T(128)}, f32[1024,4,128]{0,2,1:T(8,128)S(1)}, f32[1024,4,128]{0,2,1:T(8,128)}, f32[2,512,4,128]{3,1,2,0:T(8,128)}, s32[2]{0:T(128)S(1)}, /*i...) while((s32[]{:T(128)}, f32[1024,4,128]{0,2,1:T(8,128)S(1)}, ...), condition=%wide.region_16.17_spmd.clone.clone, body=%wide.region_14.16_spmd.clone.sunk.clone | while | flops 2719743488 | bytes 180419536 | solution.py:109
  996.9 24.7 %convolution_convert_fusion = bf16[2048,2,2048]{2,0,1:T(8,128)(2,1)} fusion(bf16[1024,1,2048]{2,0,1:T(8,128)(2,1)} %get-tuple-element.287, bf16[1024,1,2048]{2,0,1:T(8,128)(2,1)} %get-tuple-element.286, bf16[1024,2048]{1,0:T(8,128)(2,1)} %all-gather.15.cloned.1.call-done), kind=kOutput, calls=%fused_computation.49 | convolution fusion | flops 17205035008 | bytes 29360128 | tf_op jit(solution)/shard_map/td,tjf->djf/dot_general | solution.py:212
  1021.7 40.7 %psum.7 = f32[]{:T(128)} all-reduce(f32[]{:T(128)} %get-tuple-element.226), channel_id=1, replica_groups=mesh['seq'=4,'fsdp'=8] {'seq','fsdp'}, use_global_device_ids=true, to_apply=%region_21.22 | all-reduce | flops 1 | bytes 8 | tf_op jit(solution)/shard_map/psum | solution.py:190
  1068.9 31.1 %reduce-scatter.19.cloned.1.call-done = bf16[512,256]{1,0:T(8,128)(2,1)} async-done(((bf16[512,2048]{1,0:T(8,128)(2,1)}), bf16[512,256]{1,0:T(8,128)(2,1)}) %reduce-scatter.19.cloned.1.call-update) | async-done | bytes 262160 | tf_op jit(solution)/shard_map/reduce_scatter | solution.py:248
  1102.6 43.9 %reduce-scatter.15.cloned.1.call-done = bf16[256,2048]{1,0:T(8,128)(2,1)} async-done(((bf16[1024,2048]{1,0:T(8,128)(2,1)}), bf16[256,2048]{1,0:T(8,128)(2,1)}) %reduce-scatter.15.cloned.1.call-update) | async-done | bytes 1048592 | tf_op jit(solution)/shard_map/reduce_scatter | solution.py:240
  1150.4 118.1 %reduce-scatter.17.cloned.1.call-done = bf16[256,3,512]{2,0,1:T(8,128)(2,1)} async-done(((bf16[2048,3,512]{2,0,1:T(8,128)(2,1)}), bf16[256,3,512]{2,0,1:T(8,128)(2,1)}) %reduce-scatter.17.cloned.1.call-update) | async-done | bytes 786448 | tf_op jit(solution)/shard_map/reduce_scatter | solution.py:245
  1273.9 276.9 %reduce-scatter.21.cloned.1.call-done = bf16[256,2,2048]{2,0,1:T(8,128)(2,1)} async-done(((bf16[2048,2,2048]{2,0,1:T(8,128)(2,1)}), bf16[256,2,2048]{2,0,1:T(8,128)(2,1)}) %reduce-scatter.21.cloned.1.call-update) | async-done | bytes 2097168 | tf_op jit(solution)/shard_map/reduce_scatter | solution.py:251
  1550.8 13.7 fusion.44
  (262 shorter events, 260.0 us)
Async XLA Ops:
  7.2 42.5 %all-gather.9.cloned.1.call-start = ((), (), s32[]{:S(2)}) async-start(), calls=%async_computation.8 | async-start | bytes 5242880 | tf_op jit(solution)/shard_map/all_gather | solution.py:165
  12.4 139.5 %all-gather.11.cloned.1.call-start = ((), (), s32[]{:S(2)}) async-start(), calls=%async_computation.9 | async-start | bytes 7077888 | tf_op jit(solution)/shard_map/all_gather | solution.py:159
  13.6 195.1 %all-gather.13.cloned.1.call-start = ((), (), s32[]{:S(2)}) async-start(), calls=%async_computation.10 | async-start | bytes 2359296 | tf_op jit(solution)/shard_map/all_gather | solution.py:160
  14.5 243.5 %reduce-scatter.9.cloned.1.call-start = ((), (), s32[]{:S(2)}) async-start(), calls=%async_computation.11 | async-start | bytes 5242880 | tf_op jit(solution)/shard_map/reduce_scatter | solution.py:176
  204.9 10.1 copy-start.3
  215.0 81.1 %all-gather.15.cloned.1.call-start = ((), (), s32[]{:S(2)}) async-start(), calls=%async_computation.12 | async-start | bytes 5242880 | tf_op jit(solution)/shard_map/all_gather | solution.py:180
  261.6 264.5 %all-gather.17.cloned.1.call-start = ((), (), s32[]{:S(2)}) async-start(), calls=%async_computation.13 | async-start | bytes 18874368 | tf_op jit(solution)/shard_map/all_gather | solution.py:161
  267.4 384.5 %all-gather.19.cloned.1.call-start = ((), (), s32[]{:S(2)}) async-start(), calls=%async_computation.14 | async-start | bytes 9437184 | tf_op jit(solution)/shard_map/all_gather | solution.py:162
  270.3 438.2 %reduce-scatter.11.cloned.1.call-start = ((), (), s32[]{:S(2)}) async-start(), calls=%async_computation.15 | async-start | bytes 5242880 | tf_op jit(solution)/shard_map/reduce_scatter | solution.py:186
  665.6 42.9 %copy-start.17 = (bf16[1,256,2048]{2,1,0:T(8,128)(2,1)S(1)}, bf16[1,256,2048]{2,1,0:T(8,128)(2,1)}, u32[]{:S(2)}) copy-start(bf16[1,256,2048]{2,1,0:T(8,128)(2,1)} %param.20) | copy-start | bytes 3145732
  665.7 80.6 %all-gather.21.cloned.1.call-start = ((), (), s32[]{:S(2)}) async-start(), calls=%async_computation.16 | async-start | bytes 5242880 | tf_op jit(solution)/shard_map/all_gather | solution.py:200
  711.6 123.8 %reduce-scatter.13.cloned.1.call-start = ((), (), s32[]{:S(2)}) async-start(), calls=%async_computation.17 | async-start | bytes 5242880 | tf_op jit(solution)/shard_map/reduce_scatter | solution.py:213
  790.6 86.7 %all-gather.23.cloned.1.call-start = ((), (), s32[]{:S(2)}) async-start(), calls=%async_computation.18 | async-start | bytes 5242880 | tf_op jit(solution)/shard_map/all_gather | solution.py:217
  842.7 220.3 %reduce-scatter.23.cloned.1.call-start = ((), (), s32[]{:S(2)}) async-start(), calls=%async_computation.23 | async-start | bytes 9437184 | tf_op jit(solution)/shard_map/reduce_scatter | solution.py:254
  857.3 242.6 %reduce-scatter.19.cloned.1.call-start = ((), (), s32[]{:S(2)}) async-start(), calls=%async_computation.21 | async-start | bytes 2359296 | tf_op jit(solution)/shard_map/reduce_scatter | solution.py:248
  860.0 17.3 %copy-start.34 = (bf16[2,512,4,128]{3,2,1,0:T(4,128)(2,1)S(1)}, bf16[2,512,4,128]{3,2,1,0:T(4,128)(2,1)}, u32[]{:S(2)}) copy-start(bf16[2,512,4,128]{3,2,1,0:T(4,128)(2,1)} %copy.65) | copy-start | bytes 3145732
  883.3 263.2 %reduce-scatter.15.cloned.1.call-start = ((), (), s32[]{:S(2)}) async-start(), calls=%async_computation.19 | async-start | bytes 5242880 | tf_op jit(solution)/shard_map/reduce_scatter | solution.py:240
  983.9 284.5 %reduce-scatter.17.cloned.1.call-start = ((), (), s32[]{:S(2)}) async-start(), calls=%async_computation.20 | async-start | bytes 7077888 | tf_op jit(solution)/shard_map/reduce_scatter | solution.py:245
  996.9 553.9 %reduce-scatter.21.cloned.1.call-start = ((), (), s32[]{:S(2)}) async-start(), calls=%async_computation.22 | async-start | bytes 18874368 | tf_op jit(solution)/shard_map/reduce_scatter | solution.py:251
  1021.7 41.4 %copy-start.21 = (f32[2048,256]{1,0:T(8,128)S(1)}, f32[2048,256]{1,0:T(8,128)}, u32[]{:S(2)}) copy-start(f32[2048,256]{1,0:T(8,128)} %param.25) | copy-start | bytes 6291460
  1068.9 77.7 %copy-start.6 = (bf16[1,256,2048]{2,1,0:T(8,128)(2,1)S(1)}, bf16[1,256,2048]{2,1,0:T(8,128)(2,1)}, u32[]{:S(2)}) copy-start(bf16[1,256,2048]{2,1,0:T(8,128)(2,1)} %param.19) | copy-start | bytes 3145732
  1068.9 77.7 %copy-start.42 = (f32[256]{0:T(256)S(1)}, f32[256]{0:T(256)}, u32[]{:S(2)}) copy-start(f32[256]{0:T(256)} %copy-done.41) | copy-start | bytes 3076
  1068.9 77.7 %copy-start.44 = (f32[256]{0:T(256)S(1)}, f32[256]{0:T(256)}, u32[]{:S(2)}) copy-start(f32[256]{0:T(256)} %copy-done.43) | copy-start | bytes 3076
  1068.9 79.7 %copy-start.22 = (f32[256,2048]{1,0:T(8,128)S(1)}, f32[256,2048]{1,0:T(8,128)}, u32[]{:S(2)}) copy-start(f32[256,2048]{1,0:T(8,128)} %get-tuple-element.281) | copy-start | bytes 6291460
  (50 other events, 194.9 us)
Sparse Core Ops, SparseCore 0:
  12.5 37.1 all-gather.8
  52.3 99.4 all-gather.10
  154.5 48.5 all-gather.12
  215.2 42.7 reduce-scatter.8
  261.7 34.4 all-gather.14
  298.8 227.2 all-gather.16
  528.7 123.1 all-gather.18
  665.8 42.7 reduce-scatter.10
  711.7 34.4 all-gather.20
  790.8 44.5 reduce-scatter.12
  842.8 34.4 all-gather.22
  880.8 147.8 reduce-scatter.22
  1032.2 67.6 reduce-scatter.18
  1102.9 43.5 reduce-scatter.14
  1150.0 118.4 reduce-scatter.16
  1272.1 278.7 reduce-scatter.20
where the time goes:
time: 1590 us
  waiting for transfers between devices  1130 us (71%)
  matrix products  215 us (14%)
  other arithmetic  98.9 us (6%)
  local copies, waits for them, and re-layouts  78.1 us (5%)
  blocking collectives  40.7 us (3%)
  between operations  17.1 us (1%)
    reduce_scatter x1, waiting for transfers between devices, on_device(): lax.psum_scatter(grad_gateup.astype(jnp.bfloat16), 'fsdp', scatter_dimens...  277 us
    all_gather x1, waiting for transfers between devices, on_device(): lax.all_gather(low_weights[2], 'fsdp', axis=0, tiled=True)  230 us
    reduce_scatter x1, waiting for transfers between devices, on_device(): lax.psum_scatter(grad_qkv.astype(jnp.bfloat16), 'fsdp', scatter_dimension...  118 us
    all_gather x1, waiting for transfers between devices, on_device(): lax.all_gather(low_weights[0], 'fsdp', axis=0, tiled=True)  102 us
    all_gather x1, waiting for transfers between devices, on_device(): lax.all_gather(low_weights[3], 'fsdp', axis=1, tiled=True)  94.6 us
    reduce_scatter x1, waiting for transfers between devices, on_device(): lax.psum_scatter(normed_grad_two.astype(jnp.bfloat16), 'seq', scatter_dim...  44.7 us
    reduce_scatter x1, waiting for transfers between devices, on_device(): lax.psum_scatter(normed_grad_one.astype(jnp.bfloat16), 'seq', scatter_dim...  43.9 us
    reduce_scatter x1, waiting for transfers between devices, on_device(): lax.psum_scatter(attn_term.astype(jnp.bfloat16), 'seq', scatter_dimension...  42.9 us
  transfers between devices with their start and end apart: 16, of which 14 were waited for; matrix products, arithmetic and copies ran while one was open for 17% of the time, Pallas kernels for 0%

commit v1 on v0

--- a/solution.py
+++ b/solution.py
@@ -9,6 +9,28 @@
 MOMENT = 0.9
 KEEP = 0.95
 NEG = -1e30
+
+
+def in_order(parts, dim):
+    shape = list(parts.shape[1:])
+    shape[dim] *= parts.shape[0]
+    return jnp.moveaxis(parts, 0, dim).reshape(shape)
+
+
+def collected_by_bits(value, axis):
+    size = lax.axis_size(axis)
+    blocks = value[None]
+    for level in range(size.bit_length() - 1):
+        bit = 1 << level
+        partner_block = lax.ppermute(blocks, axis, [(i, i ^ bit) for i in range(size)])
+        both = jnp.stack([blocks, partner_block])
+        upper = lax.axis_index(axis) >> level & 1
+        blocks = jnp.where(upper == 0, both, both[::-1]).reshape(-1, *value.shape)
+    return blocks
+
+
+def collect(shard, axis, dim):
+    return in_order(collected_by_bits(shard, axis), dim)
 
 
 def layer_norm(values):
@@ -159,7 +181,7 @@
         lax.all_gather(low_weights[0], "fsdp", axis=0, tiled=True),
         lax.all_gather(low_weights[1], "fsdp", axis=1, tiled=True),
         lax.all_gather(low_weights[2], "fsdp", axis=0, tiled=True),
-        lax.all_gather(low_weights[3], "fsdp", axis=1, tiled=True),
+        collect(low_weights[3], "fsdp", 1),
     )
     normed_one, factor_one = layer_norm(inputs)
     group_one = lax.all_gather(normed_one.astype(jnp.bfloat16), "seq", axis=0, tiled=True)

time: 1590 us -> 1850 us (1.16)
  waiting for transfers between devices: 1130 us -> 1340 us
  other arithmetic: 98.9 us -> 130 us
    ppermute x0 -> x3, waiting for transfers between devices: none -> 437 us  [collected_by_bits(): lax.ppermute(blocks, axis, [(i, i ^ bit) for i in range(size)])]
    all_gather x1, waiting for transfers between devices: 230 us -> 0.01 us  [on_device(): lax.all_gather(low_weights[2], 'fsdp', axis=0, tiled=True)]
    all_gather x1, waiting for transfers between devices: 94.6 us -> 125 us  [on_device(): lax.all_gather(low_weights[3], 'fsdp', axis=1, tiled=True)]
    all_gather x1, waiting for transfers between devices: 25.8 us -> 0.01 us  [on_device(): lax.all_gather(normed_two.astype(jnp.bfloat16), 'seq', axis=0, tiled=True)]
  transfers between devices with their start and end apart: 16 -> 19, of which waited for: 14 -> 15; matrix products, arithmetic and copies ran while one was open for 17% -> 16% of each run, Pallas kernels for 0% -> 0%
where the time goes in v1:
time: 1850 us
  waiting for transfers between devices  1340 us (72%)
  matrix products  222 us (12%)
  other arithmetic  130 us (7%)
  local copies, waits for them, and re-layouts  85.5 us (5%)
  blocking collectives  40.8 us (2%)
    ppermute x3, waiting for transfers between devices, collected_by_bits(): lax.ppermute(blocks, axis, [(i, i ^ bit) for i in range(size)])  437 us
    reduce_scatter x1, waiting for transfers between devices, on_device(): lax.psum_scatter(grad_gateup.astype(jnp.bfloat16), 'fsdp', scatter_dimens...  277 us
    all_gather x1, waiting for transfers between devices, on_device(): lax.all_gather(low_weights[3], 'fsdp', axis=1, tiled=True)  125 us
    reduce_scatter x1, waiting for transfers between devices, on_device(): lax.psum_scatter(grad_qkv.astype(jnp.bfloat16), 'fsdp', scatter_dimension...  118 us
    all_gather x1, waiting for transfers between devices, on_device(): lax.all_gather(low_weights[0], 'fsdp', axis=0, tiled=True)  102 us
    reduce_scatter x1, waiting for transfers between devices, on_device(): lax.psum_scatter(normed_grad_two.astype(jnp.bfloat16), 'seq', scatter_dim...  44.7 us
    reduce_scatter x1, waiting for transfers between devices, on_device(): lax.psum_scatter(normed_grad_one.astype(jnp.bfloat16), 'seq', scatter_dim...  43.9 us
    reduce_scatter x1, waiting for transfers between devices, on_device(): lax.psum_scatter(attn_term.astype(jnp.bfloat16), 'seq', scatter_dimension...  42.9 us
  transfers between devices with their start and end apart: 19, of which 15 were waited for; matrix products, arithmetic and copies ran while one was open for 16% of the time, Pallas kernels for 0%

profile of v1, /device:TPU:0, one launch (start us, length us, event | category | flops | bytes accessed | tf_op | source)
XLA Modules:
  0.0 1847.6 jit_solution(13149718555216796241)
XLA Ops:
  19.5 30.2 %all-gather.9.cloned.1.call-done = bf16[1024,2048]{1,0:T(8,128)(2,1)} async-done(((bf16[256,2048]{1,0:T(8,128)(2,1)}), bf16[1024,2048]{1,0:T(8,128)(2,1)}) %all-gather.9.cloned.1.call-update) | async-done | bytes 4194320 | tf_op jit(solution)/shard_map/all_gather | solution.py:187
  49.8 102.1 %all-gather.11.cloned.1.call-done = bf16[2048,3,512]{0,2,1:T(8,128)(2,1)} async-done(((bf16[256,3,512]{0,2,1:T(8,128)(2,1)}), bf16[2048,3,512]{0,2,1:T(8,128)(2,1)}) %all-gather.11.cloned.1.call-update) | async-done | bytes 6291472 | tf_op jit(solution)/shard_map/all_gather | solution.py:181
  180.5 24.6 %while.29 = (s32[]{:T(128)}, bf16[2,512,4,128]{3,1,2,0:T(8,128)(2,1)}, f32[2,4,512]{2,1,0:T(4,128)S(1)}, s32[2]{0:T(128)S(1)}, s32[]{:T(128)}, /*index=5*/bf16[1...) while((s32[]{:T(128)}, ...), condition=%wide.region_5.6_spmd.clone, body=%wide.region_2.5_spmd.sunk.clone | while | flops 1099955712 | bytes 35199660 | solution.py:91
  215.2 42.9 %reduce-scatter.9.cloned.1.call-done = bf16[256,2048]{1,0:T(8,128)(2,1)} async-done(((bf16[1024,2048]{1,0:T(8,128)(2,1)}), bf16[256,2048]{1,0:T(8,128)(2,1)}) %reduce-scatter.9.cloned.1.call-update) | async-done | bytes 1048592 | tf_op jit(solution)/shard_map/reduce_scatter | solution.py:198
  273.4 21.6 %collective-permute-done = bf16[1,2048,256]{2,1,0:T(8,128)(2,1)} collective-permute-done((bf16[1,2048,256]{2,1,0:T(8,128)(2,1)S(1)}, bf16[1,2048,256]{2,1,0:T(8,128)(2,1)}, u32[]{:S(2)}, u32[]{:S(2)}) %collective-permute-start) | collective-permute-done | bytes 1048608 | tf_op jit(solution)/shard_map/ppermute | solution.py:25
  300.3 112.6 %collective-permute-done.1 = bf16[2,2048,256]{2,1,0:T(8,128)(2,1)} collective-permute-done((bf16[2,2048,256]{2,1,0:T(8,128)(2,1)}, bf16[2,2048,256]{2,1,0:T(8,128)(2,1)}, u32[]{:S(2)}, u32[]{:S(2)}) %collective-permute-start.1) | collective-permute-done | bytes 2097184 | tf_op jit(solution)/shard_map/ppermute | solution.py:25
  432.9 302.4 %collective-permute-done.2 = bf16[4,2048,256]{1,2,0:T(8,128)(2,1)} collective-permute-done((bf16[4,2048,256]{1,2,0:T(8,128)(2,1)}, bf16[4,2048,256]{1,2,0:T(8,128)(2,1)}, u32[]{:S(2)}, u32[]{:S(2)}) %collective-permute-start.2) | collective-permute-done | bytes 4194336 | tf_op jit(solution)/shard_map/ppermute | solution.py:25
  742.9 14.4 reverse_select_fusion
  757.3 23.5 %fusion.52 = f32[1024,2,2048]{2,0,1:T(8,128)} fusion(bf16[2048,2,2048]{2,0,1:T(8,128)(2,1)} %all-gather.17.cloned.1.call-done, bf16[1024,2048]{1,0:T(8,128)(2,1)} %all-gather.15.cloned.1.call-done), kind=kOutput, calls=%fused_computation.84 | convolution fusion | flops 17179869184 | bytes 37748736 | tf_op jit(solution)/shard_map/td,djf->tjf/dot_general | solution.py:203
  780.8 17.4 fusion.61
  803.1 38.9 %reduce-scatter.11.cloned.1.call-done = bf16[256,2048]{1,0:T(8,128)(2,1)} async-done(((bf16[1024,2048]{1,0:T(8,128)(2,1)}), bf16[256,2048]{1,0:T(8,128)(2,1)}) %reduce-scatter.11.cloned.1.call-update) | async-done | bytes 1048592 | tf_op jit(solution)/shard_map/reduce_scatter | solution.py:208
  845.1 124.5 %all-gather.21.cloned.1.call-done = bf16[2048,2048]{1,0:T(8,128)(2,1)} async-done(((bf16[2048,256]{1,0:T(8,128)(2,1)}), bf16[2048,2048]{1,0:T(8,128)(2,1)}) %all-gather.21.cloned.1.call-update) | async-done | bytes 8388624 | tf_op jit(solution)/shard_map/all_gather | solution.py:218
  969.6 34.8 %all-gather.19.cloned.1.call-done = bf16[1024,2048]{1,0:T(8,128)(2,1)} async-done(((bf16[256,2048]{1,0:T(8,128)(2,1)}), bf16[1024,2048]{1,0:T(8,128)(2,1)}) %all-gather.19.cloned.1.call-update) | async-done | bytes 4194320 | tf_op jit(solution)/shard_map/all_gather | solution.py:222
  1004.4 20.7 %fusion.60 = (bf16[1024,1,2048]{2,0,1:T(8,128)(2,1)}, bf16[1024,1,2048]{2,0,1:T(8,128)(2,1)}) fusion(f32[1024,2,2048]{2,0,1:T(8,128)} %fusion.52, bf16[1024,2048]{1,0:T(8,128)(2,1)} %all-gather.19.cloned.1.call-done, bf16[2048,2048]{1,0:T(8,128)(2,1)} %all-gather.21.cloned.1.call-done), kind=kOutput, calls=%fused_computation.93 | convolution fusion | flops 8617197568 | bytes 37748736 | tf_op jit(solution)/shard_map/dot_general | solution.py:223
  1025.1 23.8 %bitcast_convert_fusion.1 = bf16[1024,2048]{1,0:T(8,128)(2,1)} fusion(bf16[2048,2,2048]{2,0,1:T(8,128)(2,1)} %all-gather.17.cloned.1.call-done, bf16[1024,1,2048]{2,0,1:T(8,128)(2,1)} %get-tuple-element.287, bf16[1024,1,2048]{2,0,1:T(8,128)(2,1)} %get-tuple-element.286), kind=kOutput, calls=%fused_computation.54 | convolution fusion | flops 17186160640 | bytes 29360128 | tf_op jit(solution)/shard_map/tjf,djf->td/dot_general | solution.py:231
  1048.9 44.7 %reduce-scatter.13.cloned.1.call-done = bf16[256,2048]{1,0:T(8,128)(2,1)} async-done(((bf16[1024,2048]{1,0:T(8,128)(2,1)}), bf16[256,2048]{1,0:T(8,128)(2,1)}) %reduce-scatter.13.cloned.1.call-update) | async-done | bytes 1048592 | tf_op jit(solution)/shard_map/reduce_scatter | solution.py:235
  1101.1 16.2 convolution_convert_fusion.1
  1147.9 52.1 %while.30 = (s32[]{:T(128)}, f32[1024,4,128]{0,2,1:T(8,128)S(1)}, f32[1024,4,128]{0,2,1:T(8,128)}, f32[2,512,4,128]{3,1,2,0:T(8,128)}, s32[2]{0:T(128)S(1)}, /*i...) while((s32[]{:T(128)}, f32[1024,4,128]{0,2,1:T(8,128)S(1)}, ...), condition=%wide.region_16.17_spmd.clone.clone, body=%wide.region_14.16_spmd.clone.sunk.clone | while | flops 2719743488 | bytes 180419536 | solution.py:131
  1255.2 24.7 %convolution_convert_fusion = bf16[2048,2,2048]{2,0,1:T(8,128)(2,1)} fusion(bf16[1024,1,2048]{2,0,1:T(8,128)(2,1)} %get-tuple-element.287, bf16[1024,1,2048]{2,0,1:T(8,128)(2,1)} %get-tuple-element.286, bf16[1024,2048]{1,0:T(8,128)(2,1)} %all-gather.15.cloned.1.call-done), kind=kOutput, calls=%fused_computation.50 | convolution fusion | flops 17205035008 | bytes 29360128 | tf_op jit(solution)/shard_map/td,tjf->djf/dot_general | solution.py:234
  1279.9 40.8 %psum.7 = f32[]{:T(128)} all-reduce(f32[]{:T(128)} %get-tuple-element.226), channel_id=1, replica_groups=mesh['seq'=4,'fsdp'=8] {'seq','fsdp'}, use_global_device_ids=true, to_apply=%region_21.22 | all-reduce | flops 1 | bytes 8 | tf_op jit(solution)/shard_map/psum | solution.py:212
  1327.2 31.8 %reduce-scatter.19.cloned.1.call-done = bf16[512,256]{1,0:T(8,128)(2,1)} async-done(((bf16[512,2048]{1,0:T(8,128)(2,1)}), bf16[512,256]{1,0:T(8,128)(2,1)}) %reduce-scatter.19.cloned.1.call-update) | async-done | bytes 262160 | tf_op jit(solution)/shard_map/reduce_scatter | solution.py:270
  1361.7 43.9 %reduce-scatter.15.cloned.1.call-done = bf16[256,2048]{1,0:T(8,128)(2,1)} async-done(((bf16[1024,2048]{1,0:T(8,128)(2,1)}), bf16[256,2048]{1,0:T(8,128)(2,1)}) %reduce-scatter.15.cloned.1.call-update) | async-done | bytes 1048592 | tf_op jit(solution)/shard_map/reduce_scatter | solution.py:262
  1409.4 118.1 %reduce-scatter.17.cloned.1.call-done = bf16[256,3,512]{2,0,1:T(8,128)(2,1)} async-done(((bf16[2048,3,512]{2,0,1:T(8,128)(2,1)}), bf16[256,3,512]{2,0,1:T(8,128)(2,1)}) %reduce-scatter.17.cloned.1.call-update) | async-done | bytes 786448 | tf_op jit(solution)/shard_map/reduce_scatter | solution.py:267
  1533.0 277.0 %reduce-scatter.21.cloned.1.call-done = bf16[256,2,2048]{2,0,1:T(8,128)(2,1)} async-done(((bf16[2048,2,2048]{2,0,1:T(8,128)(2,1)}), bf16[256,2,2048]{2,0,1:T(8,128)(2,1)}) %reduce-scatter.21.cloned.1.call-update) | async-done | bytes 2097168 | tf_op jit(solution)/shard_map/reduce_scatter | solution.py:273
  (283 shorter events, 314.7 us)
Async XLA Ops:
  7.2 42.6 %all-gather.9.cloned.1.call-start = ((), (), s32[]{:S(2)}) async-start(), calls=%async_computation.8 | async-start | bytes 5242880 | tf_op jit(solution)/shard_map/all_gather | solution.py:187
  12.4 139.5 %all-gather.11.cloned.1.call-start = ((), (), s32[]{:S(2)}) async-start(), calls=%async_computation.9 | async-start | bytes 7077888 | tf_op jit(solution)/shard_map/all_gather | solution.py:181
  13.7 195.2 %all-gather.13.cloned.1.call-start = ((), (), s32[]{:S(2)}) async-start(), calls=%async_computation.10 | async-start | bytes 2359296 | tf_op jit(solution)/shard_map/all_gather | solution.py:182
  14.5 243.6 %reduce-scatter.9.cloned.1.call-start = ((), (), s32[]{:S(2)}) async-start(), calls=%async_computation.11 | async-start | bytes 5242880 | tf_op jit(solution)/shard_map/reduce_scatter | solution.py:198
  215.2 542.2 %all-gather.15.cloned.1.call-start = ((), (), s32[]{:S(2)}) async-start(), calls=%async_computation.12 | async-start | bytes 5242880 | tf_op jit(solution)/shard_map/all_gather | solution.py:202
  262.3 495.0 %all-gather.17.cloned.1.call-start = ((), (), s32[]{:S(2)}) async-start(), calls=%async_computation.13 | async-start | bytes 18874368 | tf_op jit(solution)/shard_map/all_gather | solution.py:183
  268.1 573.9 %reduce-scatter.11.cloned.1.call-start = ((), (), s32[]{:S(2)}) async-start(), calls=%async_computation.14 | async-start | bytes 5242880 | tf_op jit(solution)/shard_map/reduce_scatter | solution.py:208
  270.0 24.9 %collective-permute-start = (bf16[1,2048,256]{2,1,0:T(8,128)(2,1)S(1)}, bf16[1,2048,256]{2,1,0:T(8,128)(2,1)}, u32[]{:S(2)}, u32[]{:S(2)}) collective-permute-start(bf16[1,2048,256]{2,1,0:T(8,128)(2,1)S(1)} %convert_bitcast_fusion.2), channel_id=1, source_target_pairs={{0,1},{1,0},{2,3},{3,2},{4,5},{5,4},{6,7},{7,6},{8,9},{9,8},{10,11... | collective-permute-start | bytes 3145736 | tf_op jit(solution)/shard_map/ppermute | solution.py:25
  298.8 114.1 %collective-permute-start.1 = (bf16[2,2048,256]{2,1,0:T(8,128)(2,1)}, bf16[2,2048,256]{2,1,0:T(8,128)(2,1)}, u32[]{:S(2)}, u32[]{:S(2)}) collective-permute-start(bf16[2,2048,256]{2,1,0:T(8,128)(2,1)} %get-tuple-element.301), channel_id=1, source_target_pairs={{0,2},{1,3},{2,0},{3,1},{4,6},{5,7},{6,4},{7,5},{8,10},{9,11},{10,... | collective-permute-start | bytes 6291464 | tf_op jit(solution)/shard_map/ppermute | solution.py:25
  425.6 309.7 %collective-permute-start.2 = (bf16[4,2048,256]{1,2,0:T(8,128)(2,1)}, bf16[4,2048,256]{1,2,0:T(8,128)(2,1)}, u32[]{:S(2)}, u32[]{:S(2)}) collective-permute-start(bf16[4,2048,256]{1,2,0:T(8,128)(2,1)} %copy.67), channel_id=1, source_target_pairs={{0,4},{1,5},{2,6},{3,7},{4,0},{5,1},{6,2},{7,3},{8,12},{9,13},{10,... | collective-permute-start | bytes 12582920 | tf_op jit(solution)/shard_map/ppermute | solution.py:25
  798.3 171.3 %all-gather.21.cloned.1.call-start = ((), (), s32[]{:S(2)}) async-start(), calls=%async_computation.16 | async-start | bytes 9437184 | tf_op jit(solution)/shard_map/all_gather | solution.py:218
  801.1 203.3 %all-gather.19.cloned.1.call-start = ((), (), s32[]{:S(2)}) async-start(), calls=%async_computation.15 | async-start | bytes 5242880 | tf_op jit(solution)/shard_map/all_gather | solution.py:222
  845.0 248.6 %reduce-scatter.13.cloned.1.call-start = ((), (), s32[]{:S(2)}) async-start(), calls=%async_computation.17 | async-start | bytes 5242880 | tf_op jit(solution)/shard_map/reduce_scatter | solution.py:235
  1048.9 44.8 %copy-start.47 = (f32[256]{0:T(256)S(1)}, f32[256]{0:T(256)}, u32[]{:S(2)}) copy-start(f32[256]{0:T(256)} %copy-done.46) | copy-start | bytes 3076
  1048.9 86.8 %all-gather.23.cloned.1.call-start = ((), (), s32[]{:S(2)}) async-start(), calls=%async_computation.18 | async-start | bytes 5242880 | tf_op jit(solution)/shard_map/all_gather | solution.py:239
  1101.0 220.3 %reduce-scatter.23.cloned.1.call-start = ((), (), s32[]{:S(2)}) async-start(), calls=%async_computation.23 | async-start | bytes 9437184 | tf_op jit(solution)/shard_map/reduce_scatter | solution.py:276
  1117.4 241.7 %reduce-scatter.19.cloned.1.call-start = ((), (), s32[]{:S(2)}) async-start(), calls=%async_computation.21 | async-start | bytes 2359296 | tf_op jit(solution)/shard_map/reduce_scatter | solution.py:270
  1141.6 264.0 %reduce-scatter.15.cloned.1.call-start = ((), (), s32[]{:S(2)}) async-start(), calls=%async_computation.19 | async-start | bytes 5242880 | tf_op jit(solution)/shard_map/reduce_scatter | solution.py:262
  1242.4 285.1 %reduce-scatter.17.cloned.1.call-start = ((), (), s32[]{:S(2)}) async-start(), calls=%async_computation.20 | async-start | bytes 7077888 | tf_op jit(solution)/shard_map/reduce_scatter | solution.py:267
  1255.1 554.8 %reduce-scatter.21.cloned.1.call-start = ((), (), s32[]{:S(2)}) async-start(), calls=%async_computation.22 | async-start | bytes 18874368 | tf_op jit(solution)/shard_map/reduce_scatter | solution.py:273
  1327.2 78.4 %copy-start.6 = (bf16[1,256,2048]{2,1,0:T(8,128)(2,1)S(1)}, bf16[1,256,2048]{2,1,0:T(8,128)(2,1)}, u32[]{:S(2)}) copy-start(bf16[1,256,2048]{2,1,0:T(8,128)(2,1)} %param.19) | copy-start | bytes 3145732
  1327.2 78.4 %copy-start.41 = (f32[256]{0:T(256)S(1)}, f32[256]{0:T(256)}, u32[]{:S(2)}) copy-start(f32[256]{0:T(256)} %copy-done.40) | copy-start | bytes 3076
  1327.2 78.4 %copy-start.45 = (f32[256]{0:T(256)S(1)}, f32[256]{0:T(256)}, u32[]{:S(2)}) copy-start(f32[256]{0:T(256)} %copy-done.44) | copy-start | bytes 3076
  1327.2 80.5 %copy-start.21 = (f32[256,2048]{1,0:T(8,128)S(1)}, f32[256,2048]{1,0:T(8,128)}, u32[]{:S(2)}) copy-start(f32[256,2048]{1,0:T(8,128)} %get-tuple-element.281) | copy-start | bytes 6291460
  (56 other events, 348.5 us)
Sparse Core Ops, SparseCore 0:
  12.5 37.1 all-gather.8
  52.4 99.4 all-gather.10
  154.5 48.5 all-gather.12
  215.3 42.7 reduce-scatter.8
  262.4 34.4 all-gather.14
  299.5 412.3 all-gather.16
  798.4 43.5 reduce-scatter.10
  844.6 124.9 all-gather.20
  971.7 32.6 all-gather.18
  1049.0 44.5 reduce-scatter.12
  1101.1 34.4 all-gather.22
  1139.1 147.8 reduce-scatter.22
  1290.6 68.4 reduce-scatter.18
  1362.0 43.5 reduce-scatter.14
  1409.1 118.4 reduce-scatter.16
  1531.2 278.7 reduce-scatter.20
